TPU v7x, 32 devices: a whole 2x2x4 slice. The times are simulated.
32 devices in a mesh: section: 2 (over core), dp: 4 (over y, x), tensor: 4 (over z).
Axes of the slice: x: 2, y: 2, z: 4, core: 2. Of those that a mesh axis runs over, the one named last changes fastest.
Arguments:
- tokens_in: bfloat16 [512, 8192], P('dp', ('section', 'tensor')), may hold values from -70 to 70
- gain_attn: bfloat16 [8192], replicated, may hold values from 0.5 to 1.5
- w_query: bfloat16 [8192, 8192], P(None, ('section', 'tensor')), may hold values from -6 to 6
- w_keyval: bfloat16 [8192, 2048], P(None, ('section', 'tensor')), may hold values from -0.0625 to 0.0625
- w_out: bfloat16 [8192, 8192], P(('section', 'tensor')), may hold values from -0.0625 to 0.0625
- gain_mlp: bfloat16 [8192], replicated, may hold values from 0.5 to 1.5
- w_gate: bfloat16 [8192, 16384], P('dp', ('section', 'tensor')), may hold values from -0.0625 to 0.0625
- w_up: bfloat16 [8192, 16384], P('dp', ('section', 'tensor')), may hold values from -0.0625 to 0.0625
- w_down: bfloat16 [16384, 8192], P(('section', 'tensor'), 'dp'), may hold values from -0.046875 to 0.046875
Outputs:
- layer_out: bfloat16 [512, 8192], P(('section', 'tensor'), 'dp')
All inputs are finite; a program needn't handle non-finite values.
Results may differ from a plain program's by a relative error of at most 0.0068.
Values may be sent and summed in bfloat16 or wider, within the bound.
A program may use at most 128 MiB of HBM per device.

v0:
```python
import jax
import jax.numpy as jnp
from jax import lax
from jax.sharding import PartitionSpec as P

H = 64
KVH = 8
HD = 128
EPS = 1e-05
THETA = 10000.0


def rms_scale(row_data, gain_row):
    values = row_data.astype(jnp.float32)
    factor = lax.rsqrt(jnp.mean(values * values, axis=-1, keepdims=True) + EPS)
    return (values * factor * gain_row.astype(jnp.float32)).astype(jnp.bfloat16)


def rotary(values, positions):
    half_dim = values.shape[-1] // 2
    frequency = THETA ** (-jnp.arange(half_dim, dtype=jnp.float32) * 2.0 / values.shape[-1])
    angles = positions.astype(jnp.float32)[:, None] * frequency[None, :]
    cosine = jnp.cos(angles)[:, None, :]
    sine_part = jnp.sin(angles)[:, None, :]
    first_half = values[..., :half_dim]
    second = values[..., half_dim:]
    return jnp.concatenate(
        [first_half * cosine - second * sine_part, second * cosine + first_half * sine_part],
        axis=-1,
    )


def shards(tokens_in, gain_attn, w_query, w_keyval, w_out, gain_mlp, w_gate, w_up, w_down):
    group_count = lax.axis_size(("section", "tensor"))
    group_index = lax.axis_index(("section", "tensor"))
    data_index = lax.axis_index("dp")
    local_rows = tokens_in.shape[0]
    full_rows = lax.all_gather(tokens_in, ("section", "tensor"), axis=1, tiled=True)
    normed_attn = rms_scale(full_rows, gain_attn)
    heads_dev = w_query.shape[1] // HD
    group_size = H // KVH
    kv_dev = max(1, heads_dev // group_size)
    positions_local = data_index * local_rows + jnp.arange(local_rows, dtype=jnp.int32)
    query_proj = jnp.dot(normed_attn, w_query, preferred_element_type=jnp.float32)
    query_rot = rotary(query_proj.reshape(local_rows, heads_dev, HD), positions_local).astype(
        jnp.bfloat16
    )
    keyval_part = jnp.dot(normed_attn, w_keyval, preferred_element_type=jnp.float32).astype(
        jnp.bfloat16
    )
    keyval_rows = lax.all_gather(keyval_part, ("section", "tensor"), axis=1, tiled=True)
    first_kv = group_index * heads_dev // group_size
    key_cols = lax.dynamic_slice_in_dim(keyval_rows, first_kv * HD, kv_dev * HD, 1)
    value_cols = lax.dynamic_slice_in_dim(keyval_rows, KVH * HD + first_kv * HD, kv_dev * HD, 1)
    needed = jnp.concatenate([key_cols, value_cols], axis=1)
    kv_all = lax.all_gather(needed, "dp", axis=0, tiled=True)
    total_rows = kv_all.shape[0]
    key_pos = jnp.arange(total_rows, dtype=jnp.int32)
    key_rot = rotary(
        kv_all[:, : kv_dev * HD].astype(jnp.float32).reshape(total_rows, kv_dev, HD), key_pos
    ).astype(jnp.bfloat16)
    value_all = kv_all[:, kv_dev * HD :].reshape(total_rows, kv_dev, HD)
    query_grp = query_rot.reshape(local_rows, kv_dev, heads_dev // kv_dev, HD)
    scores = jnp.einsum(
        "rkgd,skd->kgrs", query_grp, key_rot, preferred_element_type=jnp.float32
    ) * HD ** (-0.5)
    allowed = key_pos[None, :] <= positions_local[:, None]
    scores = jnp.where(allowed[None, None, :, :], scores, -1e30)
    row_peak = jnp.max(scores, axis=-1, keepdims=True)
    expo_rows = jnp.exp(scores - row_peak)
    prob_rows = (expo_rows / jnp.sum(expo_rows, axis=-1, keepdims=True)).astype(jnp.bfloat16)
    attended = jnp.einsum(
        "kgrs,skd->rkgd", prob_rows, value_all, preferred_element_type=jnp.float32
    )
    attended = attended.astype(jnp.bfloat16).reshape(local_rows, heads_dev * HD)
    head_terms = jnp.dot(attended, w_out, preferred_element_type=jnp.float32)
    summed = lax.psum(head_terms, ("section", "tensor"))
    mid_full = (full_rows.astype(jnp.float32) + summed).astype(jnp.bfloat16)
    normed_mlp = rms_scale(mid_full, gain_mlp)
    mid_cols, norm_cols = (
        lax.all_to_all(mid_full, "dp", split_axis=1, concat_axis=0, tiled=True),
        lax.all_to_all(normed_mlp, "dp", split_axis=1, concat_axis=0, tiled=True),
    )
    hidden_width = w_gate.shape[1]
    row_block = norm_cols
    gate_block = jnp.dot(row_block, w_gate, preferred_element_type=jnp.float32)
    up_block = jnp.dot(row_block, w_up, preferred_element_type=jnp.float32)
    gate_both = lax.psum_scatter(
        jnp.concatenate([gate_block, up_block], axis=1), "dp", scatter_dimension=0, tiled=True
    )
    hidden_part = (jax.nn.silu(gate_both[:, :hidden_width]) * gate_both[:, hidden_width:]).astype(
        jnp.bfloat16
    )
    hidden_all = lax.all_gather(hidden_part, "dp", axis=0, tiled=True)
    out_rows = hidden_all.shape[0] // group_count
    row_block = hidden_all
    down_part = lax.psum_scatter(
        jnp.dot(row_block, w_down, preferred_element_type=jnp.float32),
        ("section", "tensor"),
        scatter_dimension=0,
        tiled=True,
    )
    resid_rows = lax.dynamic_slice_in_dim(mid_cols, group_index * out_rows, out_rows, 0)
    return (resid_rows.astype(jnp.float32) + down_part).astype(jnp.bfloat16)


def solution(mesh):
    placed = (
        P("dp", ("section", "tensor")),
        P(),
        P(None, ("section", "tensor")),
        P(None, ("section", "tensor")),
        P(("section", "tensor"), None),
        P(),
        P("dp", ("section", "tensor")),
        P("dp", ("section", "tensor")),
        P(("section", "tensor"), "dp"),
    )
    return jax.shard_map(
        shards,
        mesh=mesh,
        in_specs=placed,
        out_specs=P(("section", "tensor"), "dp"),
        check_vma=False,
    )
```

profile of v0, /device:TPU:0, one launch (start us, length us, event | category | flops | bytes accessed | tf_op | source)
XLA Modules:
  0.0 471.4 jit_solution(17559355887173237044)
XLA Ops:
  6.5 0.7 all-gather.3.cloned.1.call-update
  7.3 0.7 convert_element_type.75
  8.1 0.3 multiply_cosine_fusion.1
  8.5 32.4 %all-gather.3.cloned.1.call-done = bf16[128,8192]{1,0:T(8,128)(2,1)} async-done(((bf16[128,1024]{1,0:T(8,128)(2,1)}), bf16[128,8192]{1,0:T(8,128)(2,1)}) %all-gather.3.cloned.1.call-update) | async-done | bytes 2097168 | tf_op jit(solution)/shard_map/all_gather | solution.py:38
  40.8 2.1 fusion.3
  42.9 3.7 convolution_convert_fusion.1
  46.7 26.2 %all_gather.13 = bf16[128,2048]{1,0:T(8,128)(2,1)S(1)} all-gather(bf16[128,256]{1,0:T(8,128)(2,1)S(1)} %convolution_convert_fusion.1), channel_id=1, replica_groups=mesh['section'=2,'dp'=4,'tensor'=4] {'section','tensor'}, dimensions={1}, use_global_device_ids=true | all-gather | bytes 589824 | tf_op jit(solution)/shard_map/all_gather | solution.py:51
  72.9 9.0 %all_gather.14 = bf16[512,256]{1,0:T(8,128)(2,1)S(1)} all-gather(bf16[128,256]{1,0:T(8,128)(2,1)S(1)} %pad_maximum_fusion.1), channel_id=1, replica_groups=mesh['section'=2,'dp'=4,'tensor'=4] {'dp'}, dimensions={0}, use_global_device_ids=true | all-gather | bytes 327680 | tf_op jit(solution)/shard_map/all_gather | solution.py:56
  81.9 8.4 %convolution_bitcast_fusion = f32[16,8,8,128]{3,1,2,0:T(8,128)S(1)} fusion(bf16[8192,1024]{1,0:T(8,128)(2,1)} %param.11, bf16[128,8192]{1,0:T(8,128)(2,1)S(1)} %copy-done, f32[8192]{0:T(1024)S(1)} %convert_element_type.75, f32[128]{0:T(128)S(1)} %add_rsqrt_fusion.1), kind=kOutput, calls=%fused_computation.19 | convolution fusion | flops 2151677952 | bytes 19431936 | tf_op jit(solution)/shard_map/dot_general | solution.py:44
  90.7 1.2 fusion.27
  92.1 0.6 fusion.32
  92.7 0.3 fusion.7
  93.0 0.5 convolution_convert_fusion
  93.6 0.7 slice-done.3
  94.3 4.8 %fusion.33 = f32[128,8192]{1,0:T(8,128)} fusion(bf16[128,1024]{0,1:T(8,128)(2,1)S(1)} %bitcast.66, bf16[1024,8192]{1,0:T(8,128)(2,1)S(1)} %bitcast.58), kind=kOutput, calls=%fused_computation.64 | convolution fusion | flops 2147483648 | bytes 21233664 | tf_op jit(solution)/shard_map/dot_general | solution.py:76
  99.2 0.6 copy-done.1
  99.9 94.9 %all-reduce.2.cloned.1.call-done = f32[128,8192]{1,0:T(8,128)} async-done(((f32[128,8192]{1,0:T(8,128)}), f32[128,8192]{1,0:T(8,128)}) %all-reduce.2.cloned.1.call-update) | async-done | bytes 4194320 | tf_op jit(solution)/shard_map/psum | solution.py:77
  194.8 3.7 fusion
  198.5 0.6 fusion.2
  199.4 28.8 %all_to_all.38 = bf16[128,4,2048]{2,0,1:T(8,128)(2,1)S(1)} all-to-all(bf16[128,4,2048]{2,0,1:T(8,128)(2,1)S(1)} %bitcast.61), channel_id=1, replica_groups=mesh['section'=2,'dp'=4,'tensor'=4] {'dp'}, dimensions={1} | all-to-all | bytes 4194304 | tf_op jit(solution)/shard_map/all_to_all | solution.py:82
  228.3 4.6 fusion.35
  232.9 4.6 fusion.34
  237.5 3.8 pad_maximum_fusion
  241.4 85.1 %reduce-scatter.3.cloned.1.call-done = f32[128,4096]{1,0:T(8,128)} async-done(((f32[512,4096]{1,0:T(8,128)}), f32[128,4096]{1,0:T(8,128)}) %reduce-scatter.3.cloned.1.call-update) | async-done | bytes 2097168 | tf_op jit(solution)/shard_map/reduce_scatter | solution.py:88
  326.5 2.6 fusion.8
  329.2 35.3 %all-gather.5.cloned.1.call-done = bf16[512,2048]{1,0:T(8,128)(2,1)} async-done(((bf16[128,2048]{1,0:T(8,128)(2,1)}), bf16[512,2048]{1,0:T(8,128)(2,1)}) %all-gather.5.cloned.1.call-update) | async-done | bytes 2097168 | tf_op jit(solution)/shard_map/all_gather | solution.py:94
  364.5 10.5 %fusion.36 = f32[512,2048]{1,0:T(8,128)} fusion(bf16[512,2048]{1,0:T(8,128)(2,1)} %all-gather.5.cloned.1.call-done, bf16[2048,2048]{1,0:T(8,128)(2,1)} %param.17), kind=kOutput, calls=%fused_computation.67 | convolution fusion | flops 4294967296 | bytes 14680064 | tf_op jit(solution)/shard_map/dot_general | solution.py:98
  374.9 1.5 copy.42
  376.4 3.6 all-to-all-start
  380.0 24.9 %all-to-all-done = bf16[128,4,2048]{2,0,1:T(8,128)(2,1)S(1)} async-done(((bf16[128,4,2048]{2,0,1:T(8,128)(2,1)}), bf16[128,4,2048]{2,0,1:T(8,128)(2,1)S(1)}, u32[]{:S(2)}, u32[]{:S(2)}) %all-to-all-start) | async-done | bytes 2097184 | tf_op jit(solution)/shard_map/all_to_all | solution.py:81
  405.0 58.1 %reduce-scatter.5.cloned.1.call-done = f32[64,2048]{1,0:T(8,128)} async-done(((f32[512,2048]{1,0:T(8,128)}), f32[64,2048]{1,0:T(8,128)}) %reduce-scatter.5.cloned.1.call-update) | async-done | bytes 524304 | tf_op jit(solution)/shard_map/reduce_scatter | solution.py:97
  463.1 1.8 add_convert_fusion
  (45 shorter events, 1.2 us)
Async XLA Ops:
  6.5 34.3 %all-gather.3.cloned.1.call-start = ((), (), s32[]{:S(2)}) async-start(), calls=%async_computation.4 | async-start | bytes 2359296 | tf_op jit(solution)/shard_map/all_gather | solution.py:38
  7.3 187.5 %all-reduce.2.cloned.1.call-start = ((), (), s32[]{:S(2)}) async-start(), calls=%async_computation.5 | async-start | bytes 8388608 | tf_op jit(solution)/shard_map/psum | solution.py:77
  42.9 39.0 %copy-start = (bf16[128,8192]{1,0:T(8,128)(2,1)S(1)}, bf16[128,8192]{1,0:T(8,128)(2,1)}, u32[]{:S(2)}) copy-start(bf16[128,8192]{1,0:T(8,128)(2,1)} %all-gather.3.cloned.1.call-done) | copy-start | bytes 6291460
  81.9 11.6 %slice-start = ((s8[16777216]{0:T(1024)(128)(4,1)}), s8[4194304]{0:T(1024)(128)(4,1)S(1)}, s32[]{:S(2)}) async-start(s8[16777216]{0:T(1024)(128)(4,1)} %bitcast.57), calls=%async_computation.9 | async-start | bytes 8388608
  81.9 11.6 %slice-start.1 = ((s8[16777216]{0:T(1024)(128)(4,1)}), s8[4194304]{0:T(1024)(128)(4,1)S(1)}, s32[]{:S(2)}) async-start(s8[16777216]{0:T(1024)(128)(4,1)} %bitcast.57), calls=%async_computation.10 | async-start | bytes 8388608
  81.9 11.6 %slice-start.2 = ((s8[16777216]{0:T(1024)(128)(4,1)}), s8[4194304]{0:T(1024)(128)(4,1)S(1)}, s32[]{:S(2)}) async-start(s8[16777216]{0:T(1024)(128)(4,1)} %bitcast.57), calls=%async_computation.11 | async-start | bytes 8388608
  92.1 2.2 slice-start.3
  99.1 0.7 copy-start.1
  99.2 227.3 %reduce-scatter.3.cloned.1.call-start = ((), (), s32[]{:S(2)}) async-start(), calls=%async_computation.6 | async-start | bytes 10485760 | tf_op jit(solution)/shard_map/reduce_scatter | solution.py:88
  194.8 33.5 %slice-start.4 = ((s8[8388608]{0:T(1024)(128)(4,1)}), s8[4194304]{0:T(1024)(128)(4,1)S(1)}, s32[]{:S(2)}) async-start(s8[8388608]{0:T(1024)(128)(4,1)} %bitcast.67), calls=%async_computation.13 | async-start | bytes 8388608
  198.5 29.8 %slice-start.5 = ((s8[8388608]{0:T(1024)(128)(4,1)}), s8[4194304]{0:T(1024)(128)(4,1)S(1)}, s32[]{:S(2)}) async-start(s8[8388608]{0:T(1024)(128)(4,1)} %bitcast.67), calls=%async_computation.14 | async-start | bytes 8388608
  199.4 33.5 %slice-start.6 = ((s8[8388608]{0:T(1024)(128)(4,1)}), s8[4194304]{0:T(1024)(128)(4,1)S(1)}, s32[]{:S(2)}) async-start(s8[8388608]{0:T(1024)(128)(4,1)} %bitcast.69), calls=%async_computation.15 | async-start | bytes 8388608
  228.3 4.6 slice-start.7
  241.3 123.2 %all-gather.5.cloned.1.call-start = ((), (), s32[]{:S(2)}) async-start(), calls=%async_computation.7 | async-start | bytes 2621440 | tf_op jit(solution)/shard_map/all_gather | solution.py:94
  329.1 133.9 %reduce-scatter.5.cloned.1.call-start = ((), (), s32[]{:S(2)}) async-start(), calls=%async_computation.8 | async-start | bytes 4718592 | tf_op jit(solution)/shard_map/reduce_scatter | solution.py:97
  376.4 28.6 %all-to-all-start = ((bf16[128,4,2048]{2,0,1:T(8,128)(2,1)}), bf16[128,4,2048]{2,0,1:T(8,128)(2,1)S(1)}, u32[]{:S(2)}, u32[]{:S(2)}) async-start(bf16[128,4,2048]{2,0,1:T(8,128)(2,1)} %bitcast.59), calls=%async_computation | async-start | bytes 4194304 | tf_op jit(solution)/shard_map/all_to_all | solution.py:81
Sparse Core Ops, SparseCore 0:
  8.9 31.8 all-gather.2
  99.3 95.4 all-reduce.1
  241.4 85.0 reduce-scatter.2
  329.3 35.1 all-gather.4
  375.1 87.9 reduce-scatter.4
where the time goes:
time: 472 us; the launch traced here: 471 us
  waiting for transfers between devices  332 us (70%)
  blocking collectives  64 us (14%)
  matrix products  37.7 us (8%)
  other arithmetic  17.5 us (4%)
  between operations  13.5 us (3%)
    psum x1, waiting for transfers between devices, shards(): summed = lax.psum(head_terms, ('section', 'tensor'))  94.9 us
    reduce_scatter x1, waiting for transfers between devices, shards(): lax.psum_scatter(jnp.concatenate([gate_block, up_block], axis=1), 'dp', s...  85.1 us
    reduce_scatter x1, waiting for transfers between devices, shards(): lax.psum_scatter(jnp.dot(row_block, w_down, preferred_element_type=jnp.fl...  58.1 us
    all_gather x1, waiting for transfers between devices, shards(): hidden_all = lax.all_gather(hidden_part, 'dp', axis=0, tiled=True)  35.3 us
    all_gather x1, waiting for transfers between devices, shards(): lax.all_gather(tokens_in, ('section', 'tensor'), axis=1, tiled=True)  32.4 us
    all_to_all x1, blocking collectives, shards(): lax.all_to_all(normed_mlp, 'dp', split_axis=1, concat_axis=0, tiled=True)  28.8 us
    all_gather x1, blocking collectives, shards(): lax.all_gather(keyval_part, ('section', 'tensor'), axis=1, tiled=True)  26.2 us
    all_to_all x1, waiting for transfers between devices, shards(): lax.all_to_all(mid_full, 'dp', split_axis=1, concat_axis=0, tiled=True)  24.9 us
  transfers between devices with their start and end apart: 6, of which 6 were waited for; matrix products, arithmetic and copies ran while one was open for 1% of the time, Pallas kernels for 0%

commit v1 on v0

--- a/solution.py
+++ b/solution.py
@@ -74,7 +74,8 @@
     )
     attended = attended.astype(jnp.bfloat16).reshape(local_rows, heads_dev * HD)
     head_terms = jnp.dot(attended, w_out, preferred_element_type=jnp.float32)
-    summed = lax.psum(head_terms, ("section", "tensor"))
+    all_values = lax.all_gather(head_terms, axis_name=("section", "tensor"))
+    summed = jnp.sum(all_values, axis=0)
     mid_full = (full_rows.astype(jnp.float32) + summed).astype(jnp.bfloat16)
     normed_mlp = rms_scale(mid_full, gain_mlp)
     mid_cols, norm_cols = (

time: 472 us -> 693 us (1.47)
  waiting for transfers between devices: 332 us -> 522 us
  other arithmetic: 17.5 us -> 32.7 us
  local copies, waits for them, and re-layouts: 3.48 us -> 11.2 us
    all_gather x0 -> x1, waiting for transfers between devices: none -> 287 us  [shards(): all_values = lax.all_gather(head_terms, axis_name=('section', 'tensor'))]
    psum x1 -> x0, waiting for transfers between devices: 94.9 us -> none  [shards(): summed = lax.psum(head_terms, ('section', 'tensor'))]
    reduce_sum x0 -> x1, other arithmetic: none -> 14 us  [shards(): summed = jnp.sum(all_values, axis=0)]
  transfers between devices with their start and end apart: 6 -> 6, of which waited for: 6 -> 6; matrix products, arithmetic and copies ran while one was open for 1% -> 0% of each run, Pallas kernels for 0% -> 0%
where the time goes in v1:
time: 693 us; the launch traced here: 692 us
  waiting for transfers between devices  522 us (75%)
  blocking collectives  65.7 us (9%)
  matrix products  44 us (6%)
  other arithmetic  32.7 us (5%)
  between operations  13.4 us (2%)
  local copies, waits for them, and re-layouts  11.2 us (2%)
    all_gather x1, waiting for transfers between devices, shards(): all_values = lax.all_gather(head_terms, axis_name=('section', 'tensor'))  287 us
    reduce_scatter x1, waiting for transfers between devices, shards(): lax.psum_scatter(jnp.concatenate([gate_block, up_block], axis=1), 'dp', s...  83.1 us
    reduce_scatter x1, waiting for transfers between devices, shards(): lax.psum_scatter(jnp.dot(row_block, w_down, preferred_element_type=jnp.fl...  58.1 us
    all_gather x1, waiting for transfers between devices, shards(): hidden_all = lax.all_gather(hidden_part, 'dp', axis=0, tiled=True)  35.3 us
    all_gather x1, waiting for transfers between devices, shards(): lax.all_gather(tokens_in, ('section', 'tensor'), axis=1, tiled=True)  32.4 us
    all_to_all x1, blocking collectives, shards(): lax.all_to_all(normed_mlp, 'dp', split_axis=1, concat_axis=0, tiled=True)  30.5 us
    all_gather x1, blocking collectives, shards(): lax.all_gather(keyval_part, ('section', 'tensor'), axis=1, tiled=True)  26.2 us
    all_to_all x1, waiting for transfers between devices, shards(): lax.all_to_all(mid_full, 'dp', split_axis=1, concat_axis=0, tiled=True)  24.9 us
  transfers between devices with their start and end apart: 6, of which 6 were waited for; matrix products, arithmetic and copies ran while one was open for 0% of the time, Pallas kernels for 0%

profile of v1, /device:TPU:0, one launch (start us, length us, event | category | flops | bytes accessed | tf_op | source)
XLA Modules:
  0.0 692.4 jit_solution(8643388113371828054)
XLA Ops:
  6.5 0.7 all-gather.5.cloned.1.call-update
  7.3 0.7 convert_element_type.75
  8.5 32.4 %all-gather.5.cloned.1.call-done = bf16[128,8192]{1,0:T(8,128)(2,1)} async-done(((bf16[128,1024]{1,0:T(8,128)(2,1)}), bf16[128,8192]{1,0:T(8,128)(2,1)}) %all-gather.5.cloned.1.call-update) | async-done | bytes 2097168 | tf_op jit(solution)/shard_map/all_gather | solution.py:38
  40.8 2.1 fusion.3
  42.9 3.7 convolution_convert_fusion.1
  46.7 26.2 %all_gather.19 = bf16[128,2048]{1,0:T(8,128)(2,1)S(1)} all-gather(bf16[128,256]{1,0:T(8,128)(2,1)S(1)} %convolution_convert_fusion.1), channel_id=1, replica_groups=mesh['section'=2,'dp'=4,'tensor'=4] {'section','tensor'}, dimensions={1}, use_global_device_ids=true | all-gather | bytes 589824 | tf_op jit(solution)/shard_map/all_gather | solution.py:51
  72.9 9.0 %all_gather.20 = bf16[512,256]{1,0:T(8,128)(2,1)S(1)} all-gather(bf16[128,256]{1,0:T(8,128)(2,1)S(1)} %pad_maximum_fusion.1), channel_id=1, replica_groups=mesh['section'=2,'dp'=4,'tensor'=4] {'dp'}, dimensions={0}, use_global_device_ids=true | all-gather | bytes 327680 | tf_op jit(solution)/shard_map/all_gather | solution.py:56
  81.9 8.4 %convolution_bitcast_fusion = f32[16,8,8,128]{3,1,2,0:T(8,128)S(1)} fusion(bf16[8192,1024]{1,0:T(8,128)(2,1)} %param.11, bf16[128,8192]{1,0:T(8,128)(2,1)S(1)} %copy-done, f32[8192]{0:T(1024)S(1)} %convert_element_type.75, f32[128]{0:T(128)S(1)} %add_rsqrt_fusion.1), kind=kOutput, calls=%fused_computation.18 | convolution fusion | flops 2151677952 | bytes 19431936 | tf_op jit(solution)/shard_map/dot_general | solution.py:44
  90.7 1.2 fusion.27
  92.1 0.6 fusion.32
  93.6 0.7 slice-done.3
  94.3 4.9 fusion.33
  99.3 0.6 copy-done.2
  99.9 287.0 %all-gather.9.cloned.1.call-done = f32[1024,8192]{1,0:T(8,128)} async-done(((f32[128,8192]{1,0:T(8,128)}), f32[1024,8192]{1,0:T(8,128)}) %all-gather.9.cloned.1.call-update) | async-done | bytes 33554448 | tf_op jit(solution)/shard_map/all_gather | solution.py:77
  387.0 14.0 %reduce_sum.38 = f32[128,8192]{1,0:T(8,128)} reduce(f32[8,128,8192]{2,1,0:T(8,128)} %bitcast.53, f32[]{:T(128)} %constant.19.clone.1), dimensions={0}, to_apply=%region_3.4 | reduce | flops 7340032 | bytes 37748740 | tf_op jit(solution)/shard_map/reduce_sum | solution.py:78
  401.0 3.6 fusion
  404.6 1.9 fusion.2
  406.5 4.1 copy.32
  410.6 30.5 %all_to_all.38 = bf16[128,4,2048]{0,2,1:T(8,128)(2,1)} all-to-all(bf16[128,4,2048]{0,2,1:T(8,128)(2,1)} %bitcast.58), channel_id=1, replica_groups=mesh['section'=2,'dp'=4,'tensor'=4] {'dp'}, dimensions={1} | all-to-all | bytes 4194304 | tf_op jit(solution)/shard_map/all_to_all | solution.py:83
  441.1 4.0 copy.33
  445.1 8.5 %fusion.34 = f32[512,2048]{1,0:T(8,128)S(1)} fusion(bf16[512,2048]{1,0:T(8,128)(2,1)} %bitcast.62, bf16[2048,2048]{1,0:T(8,128)(2,1)} %param.15), kind=kOutput, calls=%fused_computation.64 | convolution fusion | flops 4294967296 | bytes 14680064 | tf_op jit(solution)/shard_map/dot_general | solution.py:87
  453.6 6.9 fusion.35
  460.5 3.8 pad_maximum_fusion
  464.3 83.1 %reduce-scatter.3.cloned.1.call-done = f32[128,4096]{1,0:T(8,128)} async-done(((f32[512,4096]{1,0:T(8,128)}), f32[128,4096]{1,0:T(8,128)}) %reduce-scatter.3.cloned.1.call-update) | async-done | bytes 2097168 | tf_op jit(solution)/shard_map/reduce_scatter | solution.py:89
  547.4 2.6 fusion.8
  550.2 35.3 %all-gather.7.cloned.1.call-done = bf16[512,2048]{1,0:T(8,128)(2,1)} async-done(((bf16[128,2048]{1,0:T(8,128)(2,1)}), bf16[512,2048]{1,0:T(8,128)(2,1)}) %all-gather.7.cloned.1.call-update) | async-done | bytes 2097168 | tf_op jit(solution)/shard_map/all_gather | solution.py:95
  585.4 10.5 %fusion.36 = f32[512,2048]{1,0:T(8,128)} fusion(bf16[512,2048]{1,0:T(8,128)(2,1)} %all-gather.7.cloned.1.call-done, bf16[2048,2048]{1,0:T(8,128)(2,1)} %param.17), kind=kOutput, calls=%fused_computation.66 | convolution fusion | flops 4294967296 | bytes 14680064 | tf_op jit(solution)/shard_map/dot_general | solution.py:99
  595.9 1.5 copy.46
  597.4 3.6 all-to-all-start
  601.0 24.9 %all-to-all-done = bf16[128,4,2048]{2,0,1:T(8,128)(2,1)S(1)} async-done(((bf16[128,4,2048]{2,0,1:T(8,128)(2,1)}), bf16[128,4,2048]{2,0,1:T(8,128)(2,1)S(1)}, u32[]{:S(2)}, u32[]{:S(2)}) %all-to-all-start) | async-done | bytes 2097184 | tf_op jit(solution)/shard_map/all_to_all | solution.py:82
  626.0 58.1 %reduce-scatter.5.cloned.1.call-done = f32[64,2048]{1,0:T(8,128)} async-done(((f32[512,2048]{1,0:T(8,128)}), f32[64,2048]{1,0:T(8,128)}) %reduce-scatter.5.cloned.1.call-update) | async-done | bytes 524304 | tf_op jit(solution)/shard_map/reduce_scatter | solution.py:98
  684.1 1.8 add_convert_fusion
  (39 shorter events, 2.0 us)
Async XLA Ops:
  6.5 34.3 %all-gather.5.cloned.1.call-start = ((), (), s32[]{:S(2)}) async-start(), calls=%async_computation.4 | async-start | bytes 2359296 | tf_op jit(solution)/shard_map/all_gather | solution.py:38
  7.3 379.7 %all-gather.9.cloned.1.call-start = ((), (), s32[]{:S(2)}) async-start(), calls=%async_computation.8 | async-start | bytes 37748736 | tf_op jit(solution)/shard_map/all_gather | solution.py:77
  42.9 39.0 %copy-start = (bf16[128,8192]{1,0:T(8,128)(2,1)S(1)}, bf16[128,8192]{1,0:T(8,128)(2,1)}, u32[]{:S(2)}) copy-start(bf16[128,8192]{1,0:T(8,128)(2,1)} %all-gather.5.cloned.1.call-done) | copy-start | bytes 6291460
  81.9 11.6 %slice-start = ((s8[16777216]{0:T(1024)(128)(4,1)}), s8[4194304]{0:T(1024)(128)(4,1)S(1)}, s32[]{:S(2)}) async-start(s8[16777216]{0:T(1024)(128)(4,1)} %bitcast.55), calls=%async_computation.9 | async-start | bytes 8388608
  81.9 11.6 %slice-start.1 = ((s8[16777216]{0:T(1024)(128)(4,1)}), s8[4194304]{0:T(1024)(128)(4,1)S(1)}, s32[]{:S(2)}) async-start(s8[16777216]{0:T(1024)(128)(4,1)} %bitcast.55), calls=%async_computation.10 | async-start | bytes 8388608
  81.9 11.6 %slice-start.2 = ((s8[16777216]{0:T(1024)(128)(4,1)}), s8[4194304]{0:T(1024)(128)(4,1)S(1)}, s32[]{:S(2)}) async-start(s8[16777216]{0:T(1024)(128)(4,1)} %bitcast.55), calls=%async_computation.11 | async-start | bytes 8388608
  92.1 2.2 slice-start.3
  99.2 0.7 copy-start.2
  99.2 448.2 %reduce-scatter.3.cloned.1.call-start = ((), (), s32[]{:S(2)}) async-start(), calls=%async_computation.5 | async-start | bytes 10485760 | tf_op jit(solution)/shard_map/reduce_scatter | solution.py:89
  445.1 8.5 %copy-start.1 = (bf16[4,128,2048]{2,1,0:T(8,128)(2,1)S(1)}, bf16[4,128,2048]{2,1,0:T(8,128)(2,1)}, u32[]{:S(2)}) copy-start(bf16[4,128,2048]{2,1,0:T(8,128)(2,1)} %copy.33) | copy-start | bytes 6291460
  464.3 121.2 %all-gather.7.cloned.1.call-start = ((), (), s32[]{:S(2)}) async-start(), calls=%async_computation.6 | async-start | bytes 2621440 | tf_op jit(solution)/shard_map/all_gather | solution.py:95
  550.1 133.9 %reduce-scatter.5.cloned.1.call-start = ((), (), s32[]{:S(2)}) async-start(), calls=%async_computation.7 | async-start | bytes 4718592 | tf_op jit(solution)/shard_map/reduce_scatter | solution.py:98
  597.4 28.6 %all-to-all-start = ((bf16[128,4,2048]{2,0,1:T(8,128)(2,1)}), bf16[128,4,2048]{2,0,1:T(8,128)(2,1)S(1)}, u32[]{:S(2)}, u32[]{:S(2)}) async-start(bf16[128,4,2048]{2,0,1:T(8,128)(2,1)} %bitcast.57), calls=%async_computation | async-start | bytes 4194304 | tf_op jit(solution)/shard_map/all_to_all | solution.py:82
Sparse Core Ops, SparseCore 0:
  8.9 31.8 all-gather.4
  99.4 287.5 all-gather.8
  464.4 83.0 reduce-scatter.2
  550.2 35.1 all-gather.6
  596.0 87.9 reduce-scatter.4
